TPU v7x, 32 devices: a 4x4x1 block of a 4x4x8 slice. The times are simulated.
32 devices in a mesh: dp: 1 (over z), ep: 32 (over y, x, core).
Axes of the slice: x: 4, y: 4, z: 1, core: 2. Of those that a mesh axis runs over, the one named last changes fastest.
The devices are a block of a 4x4x8 slice.
Arguments:
- x_rows: bfloat16 [32768, 2048], P(('dp', 'ep'))
- logits: float32 [32768, 256], P(('dp', 'ep'))
- w_in: bfloat16 [256, 2048, 512], P('ep')
- w_out: bfloat16 [256, 512, 2048], P('ep')
Outputs:
- output: bfloat16 [32768, 2048], P(('dp', 'ep'))
All inputs are finite; a program needn't handle non-finite values.
Results may differ from a plain program's by a relative error of at most 0.001.
Values are sent between devices in bfloat16 or wider.
A program may use at most 768 MiB of HBM per device.

v0:
```python
import functools

import jax
import jax.numpy as jnp
from jax import lax
from jax.experimental import pallas as pl
from jax.experimental.pallas import tpu as pltpu
from jax.sharding import PartitionSpec as P

CAP_FACTOR = 2
SLOT_FACTOR = 4
CORES = 2
SUB = 16
WEIGHT_SLOTS = 6
LANE = 128
VMEM_LIMIT = 62 * 1024 * 1024
BF16 = jnp.bfloat16
F32 = jnp.float32
I32 = jnp.int32


MESH = pl.DeviceIdType.MESH


def iota(shape, dim):
    return lax.broadcasted_iota(I32, shape, dim)


def route_kernel(sizes, capacity, exp_dev, logits_ref, row_ref, keep_ref, start_ref, cnt_ref, back_ref, pick_ref,
                 stage, counts_v, send_sem, recv_sem):
    tokens, experts = logits_ref.shape
    devs = counts_v.shape[0]
    exp_chip = CORES * exp_dev
    me = lax.axis_index('ep')
    chip = me // CORES
    core = me % CORES
    barrier = pltpu.get_barrier_semaphore()

    def other(d):
        return {'ep': (me + d) % devs}

    def hello(d, c):
        pl.semaphore_signal(barrier, inc=1, device_id=other(d), device_id_type=MESH)
        return c
    lax.fori_loop(1, devs, hello, 0)

    lt = logits_ref[...].T
    ids = iota(lt.shape, 0)
    m1 = jnp.max(lt, axis=0, keepdims=True)
    e1 = jnp.min(jnp.where(lt == m1, ids, experts), axis=0, keepdims=True)
    rest = jnp.where(ids == e1, -jnp.inf, lt)
    m2 = jnp.max(rest, axis=0, keepdims=True)
    e2 = jnp.min(jnp.where(rest == m2, ids, experts), axis=0, keepdims=True)
    hit1 = ids == e1
    hit2 = ids == e2
    chosen = jnp.where(hit1 | hit2, 1.0, 0.0).astype(BF16)
    ones = jnp.ones((8, tokens), BF16)
    count = lax.dot_general(ones, chosen, (((1,), (1,)), ((), ())), preferred_element_type=F32)
    stage[...] = count
    counts_v[me] = count
    pl.semaphore_wait(barrier, devs - 1)

    def copy(d):
        return pltpu.make_async_remote_copy(
            src_ref=stage, dst_ref=counts_v.at[me], send_sem=send_sem.at[d], recv_sem=recv_sem.at[d],
            device_id=other(d), device_id_type=MESH)

    def start_copy(d, c):
        copy(d).start()
        return c

    total = jnp.sum(jnp.exp(lt - m1), axis=0, keepdims=True)
    gates = (1.0 / total, jnp.exp(m2 - m1) / total)
    lax.fori_loop(1, devs, start_copy, 0)
    upper = jnp.where(iota((tokens, tokens), 0) < iota((tokens, tokens), 1), 1.0, 0.0).astype(BF16)
    before = jnp.dot(chosen, upper, preferred_element_type=F32)
    pos1 = jnp.sum(jnp.where(hit1, before, 0.0), axis=0, keepdims=True).astype(I32)
    pos2 = jnp.sum(jnp.where(hit2, before, 0.0), axis=0, keepdims=True).astype(I32)

    def wait_copy(d, c):
        copy(d).wait()
        return c
    lax.fori_loop(1, devs, wait_copy, 0)

    counts = counts_v[:, 0, :]
    lower = jnp.where(iota((devs, devs), 1) < iota((devs, devs), 0), 1.0, 0.0).astype(BF16)
    offs = jnp.dot(lower, counts.astype(BF16), preferred_element_type=F32)
    kept = jnp.minimum(jnp.maximum(capacity - offs, 0.0), counts)
    kept_b = kept.astype(BF16)
    row_e = iota((experts, experts), 0)
    col_e = iota((experts, experts), 1)
    same = (row_e // exp_chip == col_e // exp_chip) & (row_e < col_e)
    start = jnp.dot(kept_b, jnp.where(same, 1.0, 0.0).astype(BF16), preferred_element_type=F32)
    start_b = start.astype(BF16)
    member = jnp.where(iota((experts, LANE), 0) // exp_chip == iota((experts, LANE), 1), 1.0, 0.0).astype(BF16)
    totals = jnp.dot(kept_b, member, preferred_element_type=F32)
    most = jnp.max(jnp.max(totals, axis=0, keepdims=True), axis=1, keepdims=True).astype(I32)
    size = jnp.full((1, 1), sizes[0], I32)
    pick = jnp.zeros((1, 1), I32)
    for small, large in zip(sizes[:-1], sizes[1:]):
        size = jnp.where(most > small, large, size)
        pick = pick + jnp.where(most > small, 1, 0)
    pick_ref[...] = jnp.broadcast_to(pick, pick_ref.shape)

    mine = iota((devs, experts), 0) == me
    my_start = jnp.sum(jnp.where(mine, start, 0.0), axis=0, keepdims=True)
    my_kept = jnp.sum(jnp.where(mine, kept, 0.0), axis=0, keepdims=True)
    look = jnp.concatenate([my_start, my_kept, jnp.zeros((6, experts), F32)], axis=0).astype(BF16)
    lanes = experts // exp_chip
    for k, (e, hit, pos) in enumerate(((e1, hit1, pos1), (e2, hit2, pos2))):
        got = jnp.dot(look, jnp.where(hit, 1.0, 0.0).astype(BF16), preferred_element_type=F32).astype(I32)
        keep = pos < got[1:2, :]
        row = (e // exp_chip) * size + got[0:1, :] + pos
        row_ref[k:k + 1, :] = jnp.where(keep, row, lanes * size)
        keep_ref[k:k + 1, :] = jnp.where(keep, gates[k], 0.0)

    srcs = devs // CORES
    pick_src = jnp.where(iota((srcs, devs), 1) == CORES * iota((srcs, devs), 0) + core, 1.0, 0.0).astype(BF16)
    pick_exp = jnp.where(iota((exp_chip, experts), 1) == chip * exp_chip + iota((exp_chip, experts), 0),
                         1.0, 0.0).astype(BF16)
    contract = (((1,), (1,)), ((), ()))

    def mine_of(table):
        part = lax.dot_general(pick_exp, table, contract, preferred_element_type=F32).astype(BF16)
        return lax.dot_general(part, pick_src, contract, preferred_element_type=F32).astype(I32)
    first = mine_of(start_b)
    count = mine_of(kept_b)
    start_ref[...] = first
    cnt_ref[...] = count
    width = back_ref.shape[1]
    ids = iota((exp_chip, width), 0)
    rows = iota((exp_chip, width), 1)
    group_rows = (srcs // 2) * capslot(tokens, experts)
    for s in range(srcs):
        off = rows - first[:, s:s + 1]
        inside = (off >= 0) & (off < count[:, s:s + 1])
        back_ref[s:s + 1, :] = jnp.sum(jnp.where(inside, ids * group_rows + off, 0), axis=0, keepdims=True)


def unroll(size):
    return max(k for k in range(1, 49) if size % k == 0)


def send_kernel(size, row_ref, x_ref, out_ref, tok, x_v, rows3, stage, x_sem, sem):
    tokens, d_model = x_ref.shape
    lanes = out_ref.shape[0]
    block = 16
    parts = x_sem.shape[0]
    part = tokens // parts

    def x_copy(p):
        rows = pl.ds(p * part, part)
        return pltpu.make_async_copy(x_ref.at[rows], x_v.at[rows], x_sem.at[p])
    for p in range(parts):
        x_copy(p).start()

    def fill(i, c):
        for u in range(16):
            t = i * 16 + u
            tok[row_ref[0, t]] = t
            tok[row_ref[1, t]] = t
        return c
    lax.fori_loop(0, tokens // 16, fill, 0)

    def relayout(i, c):
        r = pl.ds(pl.multiple_of(i * block, block), block)
        rows3[r] = x_v[r].astype(F32).reshape(block, SUB, LANE).astype(BF16)
        return c
    for p in range(parts):
        x_copy(p).wait()
        lax.fori_loop(p * part // block, (p + 1) * part // block, relayout, 0)

    slots = stage.shape[0]
    step = unroll(size)

    def copy(lane, slot):
        return pltpu.make_async_copy(stage.at[slot], out_ref.at[lane], sem.at[slot])

    def lane_step(lane, c):
        slot = lane % slots

        @pl.when(lane >= slots)
        def _():
            copy(lane - slots, slot).wait()

        def rows(i, c2):
            for u in range(step):
                r = i * step + u
                t = tok[lane * size + r]
                t = t & (tokens - 1) if tokens & (tokens - 1) == 0 else jnp.clip(t, 0, tokens - 1)
                stage[slot, r] = rows3[t]
            return c2
        lax.fori_loop(0, size // step, rows, 0)
        copy(lane, slot).start()
        return c
    lax.fori_loop(0, lanes, lane_step, 0)
    for k in range(min(slots, lanes)):
        lane = lanes - min(slots, lanes) + k
        copy(lane, lane % slots).wait()


def capslot(tokens, experts):
    return SLOT_FACTOR * tokens // experts


def grid_side(chips):
    return max(k for k in range(1, chips + 1) if chips % k == 0 and k * k <= chips)


def shifts_of(chips):
    side = grid_side(chips)
    tall = chips // side
    steps = [(dy, dx) for dy in range(tall) for dx in range(side)]
    near = [s for s in steps if s != (0, 0) and 2 * s[0] != tall and 2 * s[1] != side]
    if 2 * len(near) != chips:
        near = [s for s in steps if (s[0] + s[1]) % 2 == 0]
    far = [s for s in steps if s not in near]
    turn = (tall - 1) * (side - 1) + 1

    def rank(s):
        return (0 in s, s == (0, 0), s[1] == 0, (s[0] * turn + s[1]) % 2, s[0] != s[1])
    return sorted(near, key=rank), sorted(far, key=rank)


def moe_kernel(size, cap_slot, start_ref, map_ref, send_ref, w1o, w2o, back_ref, w1p, w2p,
               recv_a, recv_b, ret_v, ze, w1_v, w2_v, x2,
               out_sem, in_sem, ret_out_sem, ret_in_sem, swap_out_sem, swap_in_sem, w_sem):
    chips = send_ref.shape[0]
    exp_dev = w1o.shape[0]
    exp_chip = CORES * exp_dev
    groups = shifts_of(chips)
    half = len(groups[0])
    side = grid_side(chips)
    tall = chips // side
    me = lax.axis_index('ep')
    chip = me // CORES
    core = me % CORES
    cy = chip // side
    cx = chip % side
    partner = {'ep': chip * CORES + (1 - core)}

    def ahead(step):
        return ((cy + step[0]) % tall) * side + (cx + step[1]) % side

    def behind(step):
        return ((cy + tall - step[0]) % tall) * side + (cx + side - step[1]) % side

    def device(c):
        return {'ep': c * CORES + core}

    barrier = pltpu.get_barrier_semaphore()
    pl.semaphore_signal(barrier, inc=1, device_id=partner, device_id_type=MESH)
    for step in groups[0] + groups[1]:
        if step != (0, 0):
            pl.semaphore_signal(barrier, inc=1, device_id=device(ahead(step)), device_id_type=MESH)
    pl.semaphore_wait(barrier, chips)

    recvs = (recv_a, recv_b)

    def dispatch(g, q):
        step = groups[g][q]
        n = g * half + q
        dst = recvs[g].at[pl.ds(q * size, size)]
        if step == (0, 0):
            return pltpu.make_async_copy(send_ref.at[chip], dst, in_sem.at[n])
        to = ahead(step)
        return pltpu.make_async_remote_copy(
            src_ref=send_ref.at[to], dst_ref=dst, send_sem=out_sem.at[n], recv_sem=in_sem.at[n],
            device_id=device(to), device_id_type=MESH)

    def swap(k, j):
        src, dst = ((w1o, w1p), (w2o, w2p))[k]
        return pltpu.make_async_remote_copy(
            src_ref=src.at[j], dst_ref=dst.at[j], send_sem=swap_out_sem.at[k, j], recv_sem=swap_in_sem.at[k, j],
            device_id=partner, device_id_type=MESH)

    def give(g, q):
        step = groups[g][q]
        n = g * half + q
        src = ret_v.at[n]
        if step == (0, 0):
            return pltpu.make_async_copy(src, back_ref.at[chip], ret_in_sem.at[n])
        return pltpu.make_async_remote_copy(
            src_ref=src, dst_ref=back_ref.at[chip], send_sem=ret_out_sem.at[n], recv_sem=ret_in_sem.at[n],
            device_id=device(behind(step)), device_id_type=MESH)

    def dispatch_start(g, late):
        for q in range(half):
            if (groups[g][q][1] == 0) == late:
                dispatch(g, q).start()

    def dispatch_end(g, q):
        if groups[g][q] == (0, 0):
            dispatch(g, q).wait()
        else:
            dispatch(g, q).wait_recv()

    dispatch_start(0, False)

    def swap_start(j, c):
        swap(0, j).start()
        swap(1, j).start()
        return c
    lax.fori_loop(0, exp_dev, swap_start, 0)

    slots = w1_v.shape[0]

    def load(a, b, j, slot):
        return (pltpu.make_async_copy(a.at[j], w1_v.at[slot], w_sem.at[0, slot]),
                pltpu.make_async_copy(b.at[j], w2_v.at[slot], w_sem.at[1, slot]))

    def load_start(p, slot, first):
        @pl.when(p < exp_dev)
        def _():
            for d in load(w1o, w2o, p, slot):
                d.start()

        @pl.when(p >= exp_dev)
        def _():
            j = p - exp_dev
            if first:
                swap(0, j).wait_recv()
                swap(1, j).wait_recv()
            for d in load(w1p, w2p, j, slot):
                d.start()

    def load_wait(slot):
        for d in load(w1o, w2o, 0, slot):
            d.wait()

    def compute(g, i, slot):
        recv = recvs[g]
        for q in range(half):
            a = start_ref[i, behind(groups[g][q])] + q * size
            v = jnp.stack([recv[a + j] for j in range(cap_slot)]).astype(F32)
            x2[pl.ds(q * cap_slot, cap_slot), :] = v.reshape(cap_slot, SUB * LANE).astype(BF16)
        h = jnp.dot(x2[...], w1_v[slot], preferred_element_type=F32)
        h = jax.nn.gelu(h, approximate=True).astype(BF16)
        z = jnp.dot(h, w2_v[slot], preferred_element_type=F32).astype(BF16).astype(F32)
        rows = half * cap_slot
        ze[pl.ds(pl.multiple_of(i * rows, rows), rows)] = z.reshape(rows, SUB, LANE).astype(BF16)

    def is_late(g, q):
        return groups[g][q][1] == 0

    def pack_back(g):
        for q in range(half):
            lane = behind(groups[g][q])
            n = g * half + q

            def rows(b, c):
                for u in range(unroll(size)):
                    r = b * unroll(size) + u
                    ret_v[n, r] = ze[map_ref[lane, r] + q * cap_slot]
                return c
            lax.fori_loop(0, size // unroll(size), rows, 0)
            if q > 0 and not is_late(g, q - 1):
                give(g, q - 1).start()
        if not is_late(g, half - 1):
            give(g, half - 1).start()

    def give_late(g):
        for q in range(half):
            if is_late(g, q):
                give(g, q).start()

    depth = slots - 1
    for p in range(depth):
        for d in load(w1o, w2o, p, p):
            d.start()
    early = [q for q in range(half) if not is_late(0, q)]
    late = [q for q in range(half) if is_late(0, q)]
    for q in early[:half // 2]:
        dispatch_end(0, q)
    dispatch_start(0, True)
    dispatch_start(1, False)
    for q in early[half // 2:] + late:
        dispatch_end(0, q)

    def first_pass(p, c):
        @pl.when(p + depth < exp_chip)
        def _():
            load_start(p + depth, (p + depth) % slots, True)

        @pl.when(p == exp_dev)
        def _():
            dispatch_start(1, True)
        slot = p % slots
        load_wait(slot)
        compute(0, (core * exp_dev + p) % exp_chip, slot)
        return c
    lax.fori_loop(0, exp_chip, first_pass, 0)
    pack_back(0)
    for q in range(half):
        dispatch_end(1, q)
    give_late(0)
    held = exp_chip - slots

    def second_pass(b, c):
        slot = (held + b) % slots

        @pl.when(b >= slots)
        def _():
            load_wait(slot)
        compute(1, (core * exp_dev + held + b) % exp_chip, slot)

        @pl.when(b < held)
        def _():
            load_start(b, slot, False)
        return c
    lax.fori_loop(0, exp_chip, second_pass, 0)
    pack_back(1)
    for q in range(half):
        give(0, q).wait_recv() if groups[0][q] != (0, 0) else give(0, q).wait()
    give_late(1)

    def swap_end(j, c):
        swap(0, j).wait_send()
        swap(1, j).wait_send()
        return c
    lax.fori_loop(0, exp_dev, swap_end, 0)
    for g in range(2):
        for q in range(half):
            if groups[g][q] != (0, 0):
                dispatch(g, q).wait_send()
                give(g, q).wait_send()
            if g == 1:
                give(g, q).wait() if groups[g][q] == (0, 0) else give(g, q).wait_recv()


def ffn_kernel(size, cap_slot, start_ref, cnt_ref, core_ref, recv_ref, w1o, w1p, w2o, w2p, out_ref,
               recv_v, ret_v, w1_v, w2_v, xe, ze, x2, recv_sem, w_sem, out_sem):
    srcs = recv_ref.shape[0]
    exp_dev = w1o.shape[0]
    exp_chip = CORES * exp_dev
    core = core_ref[0]
    block = x2.shape[0]

    def recv_copy(s):
        return pltpu.make_async_copy(recv_ref.at[s], recv_v.at[pl.ds(s * size, size)], recv_sem.at[s])

    def out_copy(s):
        return pltpu.make_async_copy(ret_v.at[s, pl.ds(0, size)], out_ref.at[s], out_sem.at[s])

    def w_start(i):
        slot = i % 2
        local = i % exp_dev

        @pl.when(i // exp_dev == core)
        def _():
            pltpu.make_async_copy(w1o.at[local], w1_v.at[slot], w_sem.at[0, slot]).start()
            pltpu.make_async_copy(w2o.at[local], w2_v.at[slot], w_sem.at[1, slot]).start()

        @pl.when(i // exp_dev != core)
        def _():
            pltpu.make_async_copy(w1p.at[local], w1_v.at[slot], w_sem.at[0, slot]).start()
            pltpu.make_async_copy(w2p.at[local], w2_v.at[slot], w_sem.at[1, slot]).start()

    def w_wait(i):
        slot = i % 2
        pltpu.make_async_copy(w1o.at[0], w1_v.at[slot], w_sem.at[0, slot]).wait()
        pltpu.make_async_copy(w2o.at[0], w2_v.at[slot], w_sem.at[1, slot]).wait()

    for s in range(srcs):
        recv_copy(s).start()
    w_start(jnp.int32(0))
    for s in range(srcs):
        recv_copy(s).wait()

    def expert(i, c):
        slot = i % 2

        @pl.when(i + 1 < exp_chip)
        def _():
            w_start(i + 1)

        def gather(s, pos):
            n = cnt_ref[i, s]

            @pl.when(n > 0)
            def _():
                a = s * size + start_ref[i, s]
                for j in range(cap_slot):
                    xe[pos + j] = recv_v[a + j]
            return pos + n
        total = lax.fori_loop(0, srcs, gather, jnp.int32(0))
        w_wait(i)

        def tile(b, c2):
            base = pl.multiple_of(b * block, block)
            for q in range(block // 16):
                v = xe[pl.ds(base + q * 16, 16)].astype(F32).reshape(16, SUB * LANE)
                x2[pl.ds(q * 16, 16), :] = v.astype(BF16)
            h = jnp.dot(x2[...], w1_v[slot], preferred_element_type=F32)
            h = jax.nn.gelu(h, approximate=True).astype(BF16)
            z = jnp.dot(h, w2_v[slot], preferred_element_type=F32).astype(BF16).astype(F32)
            ze[pl.ds(base, block)] = z.reshape(block, SUB, LANE).astype(BF16)
            return c2
        lax.fori_loop(0, (total + block - 1) // block, tile, 0)

        def scatter(s, pos):
            n = cnt_ref[i, s]

            @pl.when(n > 0)
            def _():
                a = start_ref[i, s]
                for j in range(cap_slot):
                    ret_v[s, a + j] = ze[pos + j]
            return pos + n
        lax.fori_loop(0, srcs, scatter, jnp.int32(0))
        return c
    lax.fori_loop(0, exp_chip, expert, 0)
    for s in range(srcs):
        out_copy(s).start()
    for s in range(srcs):
        out_copy(s).wait()


def combine_kernel(row_ref, gate_ref, x_ref, ret_ref, out_ref, ret_v, x_v, out_v, y3, sem, x_sem, out_sem):
    tokens, d_model = x_ref.shape
    lanes, size = ret_ref.shape[:2]
    last = lanes * size - 1
    block = 16
    parts = x_sem.shape[0]
    part = tokens // parts

    def copy(s):
        return pltpu.make_async_copy(ret_ref.at[s], ret_v.at[pl.ds(s * size, size)], sem.at[s])

    def x_copy(p):
        rows = pl.ds(p * part, part)
        return pltpu.make_async_copy(x_ref.at[rows], x_v.at[rows], x_sem.at[p])

    def out_copy(p):
        rows = pl.ds(p * part, part)
        return pltpu.make_async_copy(out_v.at[rows], out_ref.at[rows], out_sem.at[p])
    for s in range(lanes):
        copy(s).start()
    for p in range(parts):
        x_copy(p).start()
    for s in range(lanes):
        copy(s).wait()

    def step(i, c):
        base = pl.multiple_of(i * block, block)
        for u in range(block):
            t = base + u
            g1 = gate_ref[0, t]
            g2 = gate_ref[1, t]
            z1 = ret_v[jnp.minimum(row_ref[0, t], last)].astype(F32)
            z2 = ret_v[jnp.minimum(row_ref[1, t], last)].astype(F32)
            y3[u] = jnp.where(g1 > 0, g1 * z1, 0.0) + jnp.where(g2 > 0, g2 * z2, 0.0)
        r = pl.ds(base, block)
        y = y3[...].reshape(block, d_model)
        out_v[r, :] = (x_v[r, :].astype(F32) + y).astype(BF16)
        return c
    for p in range(parts):
        x_copy(p).wait()
        lax.fori_loop(p * part // block, (p + 1) * part // block, step, 0)
        out_copy(p).start()
    for p in range(parts):
        out_copy(p).wait()


def spec(space):
    return pl.BlockSpec(memory_space=space)


SMEM = pltpu.SMEM
VMEM = pltpu.VMEM
ANY = pl.ANY


def params(number=None):
    if number is None:
        return pltpu.CompilerParams(vmem_limit_bytes=VMEM_LIMIT)
    return pltpu.CompilerParams(vmem_limit_bytes=VMEM_LIMIT, collective_id=number, has_side_effects=True)


def solution(mesh):
    devs = mesh.shape['ep']
    row_spec = P(('dp', 'ep'), None)
    expert_spec = P('ep', None, None)
    classes = [[i for i in range(devs) if i % CORES == c] for c in range(CORES)]
    partner = [(i, i ^ 1) for i in range(devs)]
    dma = pltpu.SemaphoreType.DMA

    def local_step(x_rows, logits, w_in, w_out):
        tokens, d_model = x_rows.shape
        experts = logits.shape[1]
        exp_dev, _, hidden = w_in.shape
        capacity = CAP_FACTOR * tokens * devs // experts
        cap_slot = capslot(tokens, experts)
        exp_chip = CORES * exp_dev
        chips = devs // CORES
        half = chips // 2
        full = exp_chip * cap_slot
        sizes = tuple(full * k // 64 for k in (43, 48, 64))
        core = (lax.axis_index('ep').astype(I32) % CORES).reshape(1)

        row, keep, start, cnt, back_map, pick = pl.pallas_call(
            functools.partial(route_kernel, sizes, capacity, exp_dev), name='route',
            out_shape=(jax.ShapeDtypeStruct((8, tokens), I32), jax.ShapeDtypeStruct((8, tokens), F32),
                       jax.ShapeDtypeStruct((exp_chip, chips), I32), jax.ShapeDtypeStruct((exp_chip, chips), I32),
                       jax.ShapeDtypeStruct((chips, full), I32), jax.ShapeDtypeStruct((8, LANE), I32)),
            in_specs=[spec(VMEM)],
            scratch_shapes=[VMEM((8, experts), F32), VMEM((devs, 8, experts), F32), dma((devs,)), dma((devs,))],
            compiler_params=params(0))(logits)

        def pack(size, row, x_rows):
            return pl.pallas_call(
                functools.partial(send_kernel, size), name='send',
                out_shape=jax.ShapeDtypeStruct((chips, size, SUB, LANE), BF16),
                in_specs=[spec(SMEM), spec(ANY)], out_specs=spec(ANY),
                scratch_shapes=[SMEM((chips * size + 8,), I32), VMEM((tokens, d_model), BF16),
                                VMEM((tokens, SUB, LANE), BF16), VMEM((4, size, SUB, LANE), BF16),
                                dma((4,)), dma((4,))],
                compiler_params=params())(row, x_rows)

        def combine(size, row, keep, x_rows, back):
            return pl.pallas_call(
                combine_kernel, name='combine', out_shape=jax.ShapeDtypeStruct((tokens, d_model), BF16),
                in_specs=[spec(SMEM)] * 2 + [spec(ANY)] * 2, out_specs=spec(ANY),
                scratch_shapes=[VMEM((chips * size, SUB, LANE), BF16), VMEM((tokens, d_model), BF16),
                                VMEM((tokens, d_model), BF16), VMEM((16, SUB, LANE), F32),
                                dma((chips,)), dma((4,)), dma((4,))],
                compiler_params=params())(row, keep, x_rows, back)

        def fused(number, size, x_rows, w_in, w_out, row, keep, start, cnt, back_map):
            lane_shape = jax.ShapeDtypeStruct((chips, size, SUB, LANE), BF16)
            send = pack(size, row, x_rows)
            back, _, _ = pl.pallas_call(
                functools.partial(moe_kernel, size, cap_slot), name='moe',
                out_shape=(lane_shape, jax.ShapeDtypeStruct(w_in.shape, BF16),
                           jax.ShapeDtypeStruct(w_out.shape, BF16)),
                in_specs=[spec(SMEM)] * 2 + [spec(ANY)] * 3, out_specs=(spec(ANY),) * 3,
                scratch_shapes=[
                    VMEM((half * size + cap_slot, SUB, LANE), BF16),
                    VMEM((half * size + cap_slot, SUB, LANE), BF16),
                    VMEM((chips, size, SUB, LANE), BF16),
                    VMEM((exp_chip * half * cap_slot, SUB, LANE), BF16),
                    VMEM((WEIGHT_SLOTS, d_model, hidden), BF16), VMEM((WEIGHT_SLOTS, hidden, d_model), BF16),
                    VMEM((half * cap_slot, d_model), BF16),
                    dma((chips,)), dma((chips,)), dma((chips,)), dma((chips,)),
                    dma((2, exp_dev)), dma((2, exp_dev)), dma((2, WEIGHT_SLOTS))],
                compiler_params=params(number))(start, back_map, send, w_in, w_out)
            return combine(size, row, keep, x_rows, back)

        def general(size, x_rows, w_in, w_out, row, keep, start, cnt, back_map):
            w_in_p = lax.ppermute(w_in, 'ep', partner)
            w_out_p = lax.ppermute(w_out, 'ep', partner)
            send = pack(size, row, x_rows)
            recv = lax.all_to_all(send, 'ep', 0, 0, axis_index_groups=classes, tiled=True)
            rows_max = capacity + cap_slot
            ret = pl.pallas_call(
                functools.partial(ffn_kernel, size, cap_slot), name='ffn',
                out_shape=jax.ShapeDtypeStruct((chips, size, SUB, LANE), BF16),
                in_specs=[spec(SMEM)] * 3 + [spec(ANY)] * 5, out_specs=spec(ANY),
                scratch_shapes=[
                    VMEM((chips * size + cap_slot, SUB, LANE), BF16),
                    VMEM((chips, size + cap_slot, SUB, LANE), BF16),
                    VMEM((2, d_model, hidden), BF16), VMEM((2, hidden, d_model), BF16),
                    VMEM((rows_max, SUB, LANE), BF16), VMEM((rows_max, SUB, LANE), BF16),
                    VMEM((LANE, d_model), BF16), dma((chips,)), dma((2, 2)), dma((chips,))],
                compiler_params=params())(start, cnt, core, recv, w_in, w_in_p, w_out, w_out_p)
            back = lax.all_to_all(ret, 'ep', 0, 0, axis_index_groups=classes, tiled=True)
            return combine(size, row, keep, x_rows, back)

        branches = [functools.partial(fused, 1 + k, size) for k, size in enumerate(sizes[:-1])]
        branches.append(functools.partial(general, sizes[-1]))
        return lax.switch(pick[0, 0], branches, x_rows, w_in, w_out, row, keep, start, cnt, back_map)

    return jax.shard_map(local_step, mesh=mesh, in_specs=(row_spec, row_spec, expert_spec, expert_spec),
                         out_specs=row_spec, check_vma=False)
```

profile of v0, /device:TPU:104, one launch (start us, length us, event | category | flops | bytes accessed | tf_op | source)
XLA Modules:
  0.0 355.0 jit_solution(14011629955943515797)
XLA Ops:
  0.0 14.4 %route.1 = (s32[8,1024]{1,0:T(8,128)S(1)}, f32[8,1024]{1,0:T(8,128)S(1)}, s32[16,16]{1,0:T(8,128)S(1)}, s32[16,16]{1,0:T(8,128)S(1)}, s32[16,256]{1,0:T(8,128)S(1)}, /*index=5*/s32[8,128]{1,0:T(8,128)}) custom-call(f32[1024,256]{1,0:T(8,128)} %logits_ref.1), custom_call_target="tpu_custom_call" | custom-call | tf_op jit(solution)/shard_map/route/pallas_call | solution.py:601
  14.4 1.2 slice.3
  16.2 338.6 %conditional.1 = (bf16[1024,2048]{1,0:T(8,128)(2,1)}) conditional(s32[]{:T(128)} %bitcast.1, (s32[8,1024]{1,0:T(8,128)S(1)}, bf16[1024,2048]{1,0:T(8,128)(2,1)}, s32[16,16]{1,0:T(8,128)S(1)}, s32[16,256]{1,0:T(8,128)S(1)}, bf16[8,2048,512]{2,1,0:T(8,128)(2,1)}, /*index=5*/bf16[8,512,2048]{2,1,0:T(8,128)(2,1)}, ...), branch_computations={%region_0.1_spmd, %region_1.2_spmd, %region_2.3_spmd} | conditional | flops 7 | bytes 218104000 | solution.py:671
  16.2 12.8 %send.3.send_ref = bf16[16,172,16,128]{3,2,1,0:T(8,128)(2,1)} custom-call(s32[8,1024]{1,0:T(8,128)S(1)} %get-tuple-element.52.row_ref, bf16[1024,2048]{1,0:T(8,128)(2,1)} %get-tuple-element.55.x_ref), custom_call_target="tpu_custom_call" | custom-call | tf_op jit(solution)/shard_map/cond/branch_0_fun/send/pallas_call | solution.py:611
  29.0 309.4 %moe.2 = (bf16[16,172,16,128]{3,2,1,0:T(8,128)(2,1)}, bf16[8,2048,512]{2,1,0:T(8,128)(2,1)}, bf16[8,512,2048]{2,1,0:T(8,128)(2,1)}) custom-call(s32[16,16]{1,0:T(8,128)S(1)} %get-tuple-element.56.start_ref, s32[16,256]{1,0:T(8,128)S(1)} %get-tuple-element.57.map_ref, bf16[16,172,16,128]{3,2,1,0:T(8,128)(2,1)} %send.3.send_ref, ...), custom_call_target="tpu_custom_call" | custom-call | tf_op jit(solution)/shard_map/cond/branch_0_fun/moe/pallas_call | solution.py:632
  338.4 16.1 %combine.3 = bf16[1024,2048]{1,0:T(8,128)(2,1)} custom-call(s32[8,1024]{1,0:T(8,128)S(1)} %get-tuple-element.52.row_ref, f32[8,1024]{1,0:T(8,128)S(1)} %get-tuple-element.54.gate_ref, bf16[1024,2048]{1,0:T(8,128)(2,1)} %get-tuple-element.55.x_ref, bf16[16,172,16,128]{3,2,1,0:T(8,128)(2,1)} %get-tuple-element.60.ret_ref), custom_call_target="tpu_custom_call" | custom-call | tf_op jit(solution)/shard_map/cond/branch_0_fun/combine/pallas_call | solution.py:621
where the time goes:
time: 355 us
  Pallas kernels  353 us (99%)
    pallas_call x1, Pallas kernels, fused(): pl.pallas_call(functools.partial(moe_kernel, size, cap_slot), name='moe',...  309 us
    pallas_call x1, Pallas kernels, combine(): pl.pallas_call(combine_kernel, name='combine', out_shape=jax.ShapeDtypeSt...  16.1 us
    pallas_call x1, Pallas kernels, local_step(): pl.pallas_call(functools.partial(route_kernel, sizes, capacity, exp_dev),...  14.4 us
    pallas_call x1, Pallas kernels, pack(): pl.pallas_call(functools.partial(send_kernel, size), name='send', out_sha...  12.8 us

commit v1 on v0

--- a/solution.py
+++ b/solution.py
@@ -154,17 +154,13 @@
     for p in range(parts):
         x_copy(p).start()
 
-    def fill(i, c):
-        for u in range(16):
-            t = i * 16 + u
-            tok[row_ref[0, t]] = t
-            tok[row_ref[1, t]] = t
-        return c
-    lax.fori_loop(0, tokens // 16, fill, 0)
-
     def relayout(i, c):
         r = pl.ds(pl.multiple_of(i * block, block), block)
         rows3[r] = x_v[r].astype(F32).reshape(block, SUB, LANE).astype(BF16)
+        for u in range(block):
+            t = i * block + u
+            tok[row_ref[0, t]] = t
+            tok[row_ref[1, t]] = t
         return c
     for p in range(parts):
         x_copy(p).wait()
@@ -595,7 +591,7 @@
         chips = devs // CORES
         half = chips // 2
         full = exp_chip * cap_slot
-        sizes = tuple(full * k // 64 for k in (43, 48, 64))
+        sizes = tuple(full * k // 64 for k in (42, 46, 64))
         core = (lax.axis_index('ep').astype(I32) % CORES).reshape(1)
 
         row, keep, start, cnt, back_map, pick = pl.pallas_call(

time: 355 us -> 347 us (0.977)
  Pallas kernels: 353 us -> 344 us
    pallas_call x1, Pallas kernels: 309 us -> 302 us  [fused(): pl.pallas_call(functools.partial(moe_kernel, size, cap_slot), name='moe',...]
where the time goes in v1:
time: 347 us; the launch traced here: 346 us
  Pallas kernels  344 us (99%)
    pallas_call x1, Pallas kernels, fused(): pl.pallas_call(functools.partial(moe_kernel, size, cap_slot), name='moe',...  302 us
    pallas_call x1, Pallas kernels, combine(): pl.pallas_call(combine_kernel, name='combine', out_shape=jax.ShapeDtypeSt...  16.1 us
    pallas_call x1, Pallas kernels, local_step(): pl.pallas_call(functools.partial(route_kernel, sizes, capacity, exp_dev),...  14.4 us
    pallas_call x1, Pallas kernels, pack(): pl.pallas_call(functools.partial(send_kernel, size), name='send', out_sha...  11.9 us

profile of v1, /device:TPU:104, one launch (start us, length us, event | category | flops | bytes accessed | tf_op | source)
XLA Modules:
  0.0 346.5 jit_solution(1664120147496165068)
XLA Ops:
  0.0 14.4 %route.1 = (s32[8,1024]{1,0:T(8,128)S(1)}, f32[8,1024]{1,0:T(8,128)S(1)}, s32[16,16]{1,0:T(8,128)S(1)}, s32[16,16]{1,0:T(8,128)S(1)}, s32[16,256]{1,0:T(8,128)S(1)}, /*index=5*/s32[8,128]{1,0:T(8,128)}) custom-call(f32[1024,256]{1,0:T(8,128)} %logits_ref.1), custom_call_target="tpu_custom_call" | custom-call | tf_op jit(solution)/shard_map/route/pallas_call | solution.py:597
  14.4 1.2 slice.3
  16.2 330.1 %conditional.1 = (bf16[1024,2048]{1,0:T(8,128)(2,1)}) conditional(s32[]{:T(128)} %bitcast.1, (s32[8,1024]{1,0:T(8,128)S(1)}, bf16[1024,2048]{1,0:T(8,128)(2,1)}, s32[16,16]{1,0:T(8,128)S(1)}, s32[16,256]{1,0:T(8,128)S(1)}, bf16[8,2048,512]{2,1,0:T(8,128)(2,1)}, /*index=5*/bf16[8,512,2048]{2,1,0:T(8,128)(2,1)}, ...), branch_computations={%region_0.1_spmd, %region_1.2_spmd, %region_2.3_spmd} | conditional | flops 7 | bytes 218104000 | solution.py:667
  16.2 11.9 %send.3.send_ref = bf16[16,168,16,128]{3,2,1,0:T(8,128)(2,1)} custom-call(s32[8,1024]{1,0:T(8,128)S(1)} %get-tuple-element.52.row_ref, bf16[1024,2048]{1,0:T(8,128)(2,1)} %get-tuple-element.55.x_ref), custom_call_target="tpu_custom_call" | custom-call | tf_op jit(solution)/shard_map/cond/branch_0_fun/send/pallas_call | solution.py:607
  28.1 301.9 %moe.2 = (bf16[16,168,16,128]{3,2,1,0:T(8,128)(2,1)}, bf16[8,2048,512]{2,1,0:T(8,128)(2,1)}, bf16[8,512,2048]{2,1,0:T(8,128)(2,1)}) custom-call(s32[16,16]{1,0:T(8,128)S(1)} %get-tuple-element.56.start_ref, s32[16,256]{1,0:T(8,128)S(1)} %get-tuple-element.57.map_ref, bf16[16,168,16,128]{3,2,1,0:T(8,128)(2,1)} %send.3.send_ref, ...), custom_call_target="tpu_custom_call" | custom-call | tf_op jit(solution)/shard_map/cond/branch_0_fun/moe/pallas_call | solution.py:628
  330.0 16.1 %combine.3 = bf16[1024,2048]{1,0:T(8,128)(2,1)} custom-call(s32[8,1024]{1,0:T(8,128)S(1)} %get-tuple-element.52.row_ref, f32[8,1024]{1,0:T(8,128)S(1)} %get-tuple-element.54.gate_ref, bf16[1024,2048]{1,0:T(8,128)(2,1)} %get-tuple-element.55.x_ref, bf16[16,168,16,128]{3,2,1,0:T(8,128)(2,1)} %get-tuple-element.60.ret_ref), custom_call_target="tpu_custom_call" | custom-call | tf_op jit(solution)/shard_map/cond/branch_0_fun/combine/pallas_call | solution.py:617
